TPU v7x, 256 devices: a whole 4x4x8 slice. The times are simulated.
256 devices in a mesh: seq: 32 (over y, z), mp: 8 (over x, core).
Axes of the slice: x: 4, y: 4, z: 8, core: 2. Of those that a mesh axis runs over, the one named last changes fastest.
Arguments:
- tokens: bfloat16 [12288, 2048], P('seq'), may hold values from -24 to 24
- database: bfloat16 [256, 96, 896], P('seq'), may hold values from -24 to 24
- nb_shard: int32 [192, 2], replicated, may hold values from 0 to 31, all different within a row; in each aligned block of 6 rows (0 to 5, 6 to 11, ...) no two rows name the same one
- nb_row: int32 [192, 2], replicated, may hold values from 0 to 7
- dec_gain: float32 [2048], replicated, may hold values from 0.1 to 1.9
- enc_gain: float32 [896], replicated, may hold values from 0.1 to 1.9
- w_in: bfloat16 [896, 1792], replicated, may hold values from -0.1875 to 0.1875
- w_out: bfloat16 [1792, 896], replicated, may hold values from -0.125 to 0.125
- w_query: bfloat16 [2048, 2048], P(None, 'mp'), may hold values from -0.125 to 0.125
- w_key: bfloat16 [896, 2048], P(None, 'mp'), may hold values from -0.1875 to 0.1875
- w_value: bfloat16 [896, 2048], P(None, 'mp'), may hold values from -0.1875 to 0.1875
- w_proj: bfloat16 [2048, 2048], P('mp'), may hold values from -0.5 to 0.5
- grad_out: bfloat16 [12288, 2048], P('seq'), may hold values from -6 to 6
Outputs:
- cca: bfloat16 [12288, 2048], P('seq', 'mp')
- grad_tokens: float32 [12288, 2048], P('seq', 'mp')
- grad_database: float32 [256, 96, 896], P('seq', 'mp')
Inputs may be any that keep to these rules, and one draw needn't show every extreme that they name: `nb_shard`: in each aligned block of 6 stretches (the stretches of one device) no shard is named more than 1 times, and some block reaches it; the 2 neighbours of a stretch come from different shards.
All inputs are finite; a program needn't handle non-finite values.
Results may differ from a plain program's by a relative error of at most 0.017.
Values may be sent and summed in bfloat16 or wider, within the bound.
A program may use at most 128 MiB of HBM per device.

v0:
```python
import jax
import jax.numpy as jnp
from jax import lax
from jax.sharding import Mesh
from jax.sharding import PartitionSpec as P

HD = 128
L = 96
STRETCH = 64
K = 2
SEQ_LEN = 4096
MP = ("mp_0", "mp_1")
EPSILON = 1e-06


def cut_rows(length, count):
    unit = 8 if length >= 8 * count else 1
    return [length // unit * k // count * unit for k in range(1, count)]


def gather_in_order(x, axes, sequence):
    tiles = x[None]
    for k in sequence:
        tiles = lax.all_gather(tiles, axes[k], axis=0, tiled=True)
    block = [lax.axis_size(axes[k]) for k in reversed(sequence)]
    tiles = tiles.reshape(*block, *x.shape)
    turned = sorted(range(len(sequence)), key=lambda place: sequence[len(sequence) - 1 - place])
    return tiles.transpose(*turned, *range(len(sequence), tiles.ndim)).reshape(-1, *x.shape)


def joined_along(tiles, dim):
    shape = list(tiles.shape[1:])
    shape[dim] *= tiles.shape[0]
    return jnp.moveaxis(tiles, 0, dim).reshape(shape)


def spread_gather(x, axes, dim):
    widest = max(range(max(1, x.ndim - 1)), key=lambda d: x.shape[d])
    count, outs = (len(axes), [])
    for leading, section in enumerate(jnp.split(x, cut_rows(x.shape[widest], count), axis=widest)):
        if section.size:
            sequence = [(leading - k) % count for k in range(count)]
            outs.append(gather_in_order(section, axes, sequence))
    return joined_along(jnp.concatenate(outs, axis=widest + 1), dim)


def split_up(x, dim, devices):
    shape = x.shape
    tiles = x.reshape(*shape[:dim], devices, shape[dim] // devices, *shape[dim + 1 :])
    return jnp.moveaxis(tiles, dim, 0)


def summed_on_arrival(x, axis, dim):
    devices = lax.axis_size(axis)
    tiles = lax.all_to_all(split_up(x, dim, devices), axis, 0, 0, tiled=True)
    return jnp.sum(tiles.astype(jnp.float32), axis=0)


def in_one_piece(arrays, axis, dim, along):
    both = jnp.concatenate(arrays, axis=along)
    out, at, outs = (lax.psum_scatter(both, axis, scatter_dimension=dim, tiled=True), 0, [])
    for a in arrays:
        outs.append(lax.slice_in_dim(out, at, at + a.shape[along], axis=along))
        at += a.shape[along]
    return tuple(outs)


def rms_scaling(values):
    return lax.rsqrt(jnp.mean(values * values, axis=-1, keepdims=True) + EPSILON)


def silu_slope(pre_act):
    sigmoid = jax.nn.sigmoid(pre_act)
    return sigmoid * (1.0 + pre_act * (1.0 - sigmoid))


def dot_t(matrix, weight):
    return lax.dot_general(
        matrix, weight, (((1,), (1,)), ((), ())), preferred_element_type=jnp.float32
    )


def encode(embedded, enc_gain, w_in, w_out):
    values = embedded.astype(jnp.float32)
    scaling = rms_scaling(values)
    normed = (values * scaling * enc_gain).astype(jnp.bfloat16)
    pre_act = jnp.einsum("nle,ef->nlf", normed, w_in, preferred_element_type=jnp.float32)
    hidden = jax.nn.silu(pre_act).astype(jnp.bfloat16)
    mixed = jnp.einsum("nlf,fe->nle", hidden, w_out, preferred_element_type=jnp.float32)
    encoded = (values + mixed).astype(jnp.bfloat16)
    return (encoded, pre_act, scaling)


def encode_back(embedded, pre_act, scaling, grad_enc, enc_gain, w_in, w_out):
    grad_hidden = jnp.einsum(
        "nle,fe->nlf", grad_enc.astype(jnp.bfloat16), w_out, preferred_element_type=jnp.float32
    )
    grad_pre = (grad_hidden * silu_slope(pre_act)).astype(jnp.bfloat16)
    grad_unit = (
        jnp.einsum("nlf,ef->nle", grad_pre, w_in, preferred_element_type=jnp.float32) * enc_gain
    )
    unit_rows = embedded.astype(jnp.float32) * scaling
    return grad_enc + scaling * (
        grad_unit - unit_rows * jnp.mean(grad_unit * unit_rows, axis=-1, keepdims=True)
    )


def body(
    tokens,
    database,
    nb_shard,
    nb_row,
    dec_gain,
    enc_gain,
    w_in,
    w_out,
    w_query,
    w_key,
    w_value,
    w_proj,
    grad_out,
):
    seq_count = lax.axis_size("seq")
    my_seq = lax.axis_index("seq")
    mp_count = lax.axis_size(MP)
    my_mp = lax.axis_index(MP)
    tok_rows = tokens.shape[0]
    stretches_here = tok_rows // STRETCH
    width = w_query.shape[1]
    heads_here = width // HD
    nb_here = stretches_here * K
    slot_cap = max(1, (nb_here + seq_count - 1) // seq_count)
    slot_count = seq_count * slot_cap
    tok_span = database.shape[1] // mp_count
    tok_start = my_mp * tok_span
    requests = nb_shard.reshape(seq_count, nb_here)
    req_rows = nb_row.reshape(seq_count, nb_here)
    req_order = jnp.arange(nb_here)
    same_shard = requests[:, :, None] == requests[:, None, :]
    before = req_order[None, :] < req_order[:, None]
    slot_rank = jnp.sum((same_shard & before[None]).astype(jnp.int32), axis=2)
    held_here = requests == my_seq
    slot_ids = jnp.arange(slot_cap)
    slot_pick = held_here[:, None, :] & (slot_rank[:, None, :] == slot_ids[None, :, None])
    slot_row = jnp.sum(slot_pick.astype(jnp.int32) * req_rows[:, None, :], axis=2).reshape(
        slot_count
    )
    slot_live = jnp.any(slot_pick, axis=2).reshape(slot_count)
    own_req = lax.dynamic_index_in_dim(requests, my_seq, 0, keepdims=False)
    own_rank = lax.dynamic_index_in_dim(slot_rank, my_seq, 0, keepdims=False)
    source = own_req * slot_cap + own_rank
    kv_weight = jnp.concatenate([w_key, w_value], axis=1)
    own_slice = lax.dynamic_slice_in_dim(database, tok_start, tok_span, 1)
    outgoing = jnp.take(own_slice, slot_row, axis=0)
    arrived = lax.all_to_all(outgoing, "seq", split_axis=0, concat_axis=0, tiled=True)
    embed_part = jnp.take(arrived, source, axis=0)
    enc_part, pre_part, scale_part = encode(embed_part, enc_gain, w_in, w_out)
    kv_rows = jnp.einsum(
        "nle,ef->nlf", spread_gather(enc_part, MP, 1), kv_weight, preferred_element_type=jnp.float32
    ).astype(jnp.bfloat16)
    key_rows = kv_rows[:, :, :width]
    value_rows = kv_rows[:, :, width:]
    tok_vals = tokens.astype(jnp.float32)
    tok_scaling = rms_scaling(tok_vals)
    tok_unit = tok_vals * tok_scaling
    tok_normed = (tok_unit * dec_gain).astype(jnp.bfloat16)
    query_rows = jnp.dot(tok_normed, w_query, preferred_element_type=jnp.float32).astype(
        jnp.bfloat16
    )
    query_blk = query_rows.reshape(stretches_here, STRETCH, heads_here, HD)
    key_blk = key_rows.reshape(stretches_here, K * L, heads_here, HD)
    value_blk = value_rows.reshape(stretches_here, K * L, heads_here, HD)
    factor = HD ** (-0.5)
    scores = (
        jnp.einsum("cqhd,ckhd->chqk", query_blk, key_blk, preferred_element_type=jnp.float32)
        * factor
    )
    exp_score = jnp.exp(scores)
    attn_prob = exp_score / jnp.sum(exp_score, axis=-1, keepdims=True)
    attn_weight = attn_prob.astype(jnp.bfloat16)
    context = (
        jnp.einsum("chqk,ckhd->cqhd", attn_weight, value_blk, preferred_element_type=jnp.float32)
        .astype(jnp.bfloat16)
        .reshape(tok_rows, width)
    )
    stretch_pos = (my_seq * stretches_here + jnp.arange(stretches_here)) % (SEQ_LEN // STRETCH)
    live_tok = jnp.repeat(stretch_pos != 0, STRETCH)[:, None]
    out_terms = jnp.where(
        live_tok, jnp.dot(context, w_proj, preferred_element_type=jnp.float32), 0.0
    )
    masked = jnp.where(live_tok, grad_out, jnp.zeros_like(grad_out))
    grad_ctx = dot_t(masked, w_proj).astype(jnp.bfloat16)
    grad_blk = grad_ctx.reshape(stretches_here, STRETCH, heads_here, HD)
    grad_prob = jnp.einsum(
        "cqhd,ckhd->chqk", grad_blk, value_blk, preferred_element_type=jnp.float32
    )
    grad_score = (
        attn_prob * (grad_prob - jnp.sum(attn_prob * grad_prob, axis=-1, keepdims=True)) * factor
    ).astype(jnp.bfloat16)
    grad_value = jnp.einsum(
        "chqk,cqhd->ckhd", attn_weight, grad_blk, preferred_element_type=jnp.float32
    ).astype(jnp.bfloat16)
    grad_query = (
        jnp.einsum("chqk,ckhd->cqhd", grad_score, key_blk, preferred_element_type=jnp.float32)
        .astype(jnp.bfloat16)
        .reshape(tok_rows, width)
    )
    grad_key = jnp.einsum(
        "chqk,cqhd->ckhd", grad_score, query_blk, preferred_element_type=jnp.float32
    ).astype(jnp.bfloat16)
    key_grad = grad_key.reshape(nb_here, L, width)
    value_grad = grad_value.reshape(nb_here, L, width)
    enc_terms = jnp.einsum("nlf,ef->nle", key_grad, w_key, preferred_element_type=jnp.float32)
    enc_terms = enc_terms + jnp.einsum(
        "nlf,ef->nle", value_grad, w_value, preferred_element_type=jnp.float32
    )
    grad_enc = summed_on_arrival(enc_terms.astype(jnp.bfloat16), MP, 1)
    grad_normed = dot_t(grad_query, w_query)
    tok_grad = grad_normed * dec_gain
    tok_terms = tok_scaling * (
        tok_grad - tok_unit * jnp.mean(tok_grad * tok_unit, axis=-1, keepdims=True)
    )
    grad_embed = encode_back(embed_part, pre_part, scale_part, grad_enc, enc_gain, w_in, w_out)
    place_back = (source[:, None] == jnp.arange(slot_count)[None, :]).astype(jnp.float32)
    returned = jnp.einsum("ns,nle->sle", place_back, grad_embed, precision=lax.Precision.HIGHEST)
    received = lax.all_to_all(
        returned.astype(jnp.bfloat16), "seq", split_axis=0, concat_axis=0, tiled=True
    ).astype(returned.dtype)
    row_hit = (
        (slot_row[None, :] == jnp.arange(database.shape[0])[:, None]) & slot_live[None, :]
    ).astype(jnp.float32)
    grad_database = jnp.einsum("rs,sle->rle", row_hit, received, precision=lax.Precision.HIGHEST)
    cca_sum, grad_sum = tuple(
        (
            part.astype(jnp.float32)
            for part in in_one_piece(
                (out_terms.astype(jnp.bfloat16), tok_terms.astype(jnp.bfloat16)), MP, 1, 0
            )
        )
    )
    return (cca_sum.astype(jnp.bfloat16), grad_sum, grad_database)


def solution(mesh):
    split = Mesh(mesh.devices.reshape(mesh.shape["seq"], 4, 2), ("seq", "mp_0", "mp_1"))
    placed = (
        P("seq", None),
        P("seq", None, None),
        P(),
        P(),
        P(),
        P(),
        P(),
        P(),
        P(None, MP),
        P(None, MP),
        P(None, MP),
        P(MP, None),
        P("seq", None),
    )
    return jax.shard_map(
        body,
        mesh=split,
        in_specs=placed,
        out_specs=(P("seq", MP), P("seq", MP), P("seq", MP, None)),
        check_vma=False,
    )
```

profile of v0, /device:TPU:32, one launch (start us, length us, event | category | flops | bytes accessed | tf_op | source)
XLA Modules:
  0.0 251.1 jit_solution(8221677842646894722)
XLA Ops:
  16.6 11.5 %all-to-all-start = ((bf16[32,12,896]{2,1,0:T(8,128)(2,1)}), bf16[32,12,896]{2,1,0:T(8,128)(2,1)}, u32[]{:S(2)}, u32[]{:S(2)}) async-start(bf16[32,12,896]{2,1,0:T(8,128)(2,1)} %broadcast_select_fusion), calls=%async_computation | async-start | bytes 1835008 | tf_op jit(solution)/shard_map/all_to_all | solution.py:155
  37.7 16.4 %all-to-all-done = bf16[32,12,896]{2,1,0:T(8,128)(2,1)} async-done(((bf16[32,12,896]{2,1,0:T(8,128)(2,1)}), bf16[32,12,896]{2,1,0:T(8,128)(2,1)}, u32[]{:S(2)}, u32[]{:S(2)}) %all-to-all-start) | async-done | bytes 688160 | tf_op jit(solution)/shard_map/all_to_all | solution.py:155
  62.7 13.6 %all-gather = bf16[24,12,896]{2,1,0:T(8,128)(2,1)S(1)} all-gather(bf16[6,12,896]{2,1,0:T(8,128)(2,1)S(1)} %get-tuple-element.9), channel_id=2, replica_groups=mesh['seq'=32,'mp_0'=4,'mp_1'=2] {'mp_0'}, dimensions={0}, use_global_device_ids=true | all-gather | bytes 645120 | tf_op jit(solution)/shard_map/all_gather | solution.py:24
  76.2 2.8 %all_gather.13 = bf16[8,6,12,896]{3,2,1,0:T(8,128)(2,1)S(1)} all-gather(bf16[4,6,12,896]{3,2,1,0:T(8,128)(2,1)S(1)} %bitcast.93), channel_id=1, replica_groups=mesh['seq'=32,'mp_0'=4,'mp_1'=2] {'mp_1'}, dimensions={0}, use_global_device_ids=true | all-gather | bytes 1548288 | tf_op jit(solution)/shard_map/all_gather | solution.py:24
  79.2 17.9 %all_gather.15 = bf16[8,6,12,896]{3,2,0,1:T(8,128)(2,1)S(1)} all-gather(bf16[2,6,12,896]{3,2,0,1:T(8,128)(2,1)S(1)} %copy.99), channel_id=1, replica_groups=mesh['seq'=32,'mp_0'=4,'mp_1'=2] {'mp_0'}, dimensions={0}, use_global_device_ids=true | all-gather | bytes 1290240 | tf_op jit(solution)/shard_map/all_gather | solution.py:24
  99.1 4.6 %reshape.204 = bf16[12,96,896]{2,1,0:T(8,128)(2,1)} reshape(bf16[12,8,12,896]{3,2,1,0:T(8,128)(2,1)} %maximum_bitcast_fusion) | data formatting | bytes 4128768 | tf_op jit(solution)/shard_map/reshape | solution.py:34
  103.7 3.2 %convolution_convert_fusion = bf16[12,96,512]{2,1,0:T(8,128)(2,1)S(1)} fusion(bf16[12,96,896]{2,1,0:T(8,128)(2,1)} %reshape.204, bf16[896,256]{1,0:T(8,128)(2,1)} %param.23, bf16[896,256]{1,0:T(8,128)(2,1)} %param.22), kind=kOutput, calls=%fused_computation.36 | convolution fusion | flops 1059389440 | bytes 4161536 | tf_op jit(solution)/shard_map/nle,ef->nlf/dot_general | solution.py:158
  108.0 2.5 %reshape.207 = bf16[6,192,2,128]{3,2,1,0:T(2,128)(2,1)} reshape(bf16[12,96,256]{2,1,0:T(8,128)(2,1)} %get-tuple-element.6) | data formatting | bytes 1179648 | tf_op jit(solution)/shard_map/reshape | solution.py:171
  110.6 2.6 %fusion.87 = f32[6,2,64,192]{3,2,1,0:T(8,128)} fusion(bf16[6,192,2,128]{3,2,1,0:T(2,128)(2,1)} %reshape.207, bf16[6,64,2,128]{3,2,1,0:T(2,128)(2,1)} %reshape.206), kind=kOutput, calls=%fused_computation.92 | convolution fusion | flops 38044608 | bytes 1376256 | tf_op jit(solution)/shard_map/div | solution.py:179
  113.2 2.6 %fusion.32 = f32[6,2,64,192]{3,2,1,0:T(8,128)} fusion(bf16[6,192,2,128]{3,2,1,0:T(2,128)(2,1)} %reshape.207, bf16[6,64,2,128]{3,2,1,0:T(2,128)(2,1)} %reshape.206), kind=kOutput, calls=%fused_computation.44 | convolution fusion | flops 37896192 | bytes 1376256 | tf_op jit(solution)/shard_map/cqhd,ckhd->chqk/dot_general | solution.py:175
  115.8 2.5 reshape.205
  118.3 2.6 %fusion.53 = bf16[6,64,2,128]{3,1,2,0:T(8,128)(2,1)} fusion(bf16[6,192,2,128]{3,2,1,0:T(2,128)(2,1)} %reshape.205, f32[6,2,64,192]{3,2,1,0:T(8,128)} %fusion.32), kind=kOutput, calls=%fused_computation.57 | convolution fusion | flops 38142912 | bytes 1376256 | tf_op jit(solution)/shard_map/chqk,ckhd->cqhd/dot_general | solution.py:182
  120.9 2.6 %fusion.78 = f32[6,2,64,192]{3,2,1,0:T(8,128)} fusion(bf16[6,192,2,128]{3,2,1,0:T(2,128)(2,1)} %reshape.205, bf16[6,64,2,128]{3,2,1,0:T(2,128)(2,1)} %reshape.209), kind=kOutput, calls=%fused_computation.83 | convolution fusion | flops 37748736 | bytes 1376256 | tf_op jit(solution)/shard_map/cqhd,ckhd->chqk/dot_general | solution.py:194
  123.4 3.2 %fusion.54 = bf16[6,64,2,128]{3,1,2,0:T(8,128)(2,1)} fusion(f32[6,2,64,192]{3,2,1,0:T(8,128)} %fusion.87, f32[6,2,64,192]{3,2,1,0:T(8,128)} %fusion.78, bf16[6,192,2,128]{3,2,1,0:T(2,128)(2,1)} %reshape.207), kind=kOutput, calls=%fused_computation.58 | convolution fusion | flops 38585280 | bytes 1966080 | tf_op jit(solution)/shard_map/chqk,ckhd->cqhd/dot_general | solution.py:204
  134.4 3.3 %fusion.42 = bf16[6,192,2,128]{3,1,2,0:T(8,128)(2,1)} fusion(f32[6,2,64,192]{3,2,1,0:T(8,128)} %fusion.87, f32[6,2,64,192]{3,2,1,0:T(8,128)} %fusion.78, bf16[6,64,2,128]{3,2,1,0:T(2,128)(2,1)} %reshape.206), kind=kOutput, calls=%fused_computation.50 | convolution fusion | flops 38781888 | bytes 1966080 | tf_op jit(solution)/shard_map/chqk,cqhd->ckhd/dot_general | solution.py:208
  137.8 2.5 copy.109
  140.3 2.8 %reshape.211 = bf16[12,96,256]{2,1,0:T(8,128)(2,1)} reshape(bf16[6,192,2,128]{3,2,1,0:T(2,128)(2,1)} %copy.109) | data formatting | bytes 1179648 | tf_op jit(solution)/shard_map/reshape | solution.py:211
  143.1 2.8 %fusion.43 = bf16[6,192,2,128]{3,1,2,0:T(8,128)(2,1)} fusion(bf16[6,64,2,128]{3,2,1,0:T(2,128)(2,1)} %reshape.209, f32[6,2,64,192]{3,2,1,0:T(8,128)} %fusion.32), kind=kOutput, calls=%fused_computation.51 | convolution fusion | flops 38339520 | bytes 1376256 | tf_op jit(solution)/shard_map/chqk,cqhd->ckhd/dot_general | solution.py:200
  145.9 2.5 copy.111
  148.4 2.8 %reshape.212 = bf16[12,96,256]{2,1,0:T(8,128)(2,1)} reshape(bf16[6,192,2,128]{3,2,1,0:T(2,128)(2,1)} %copy.111) | data formatting | bytes 1179648 | tf_op jit(solution)/shard_map/reshape | solution.py:212
  155.4 4.5 %reshape.213 = bf16[12,8,12,896]{3,2,1,0:T(8,128)(2,1)} reshape(bf16[12,96,896]{2,1,0:T(8,128)(2,1)} %add_convert_fusion) | data formatting | bytes 4128768 | tf_op jit(solution)/shard_map/reshape | solution.py:49
  162.0 36.9 %all_to_all.15 = bf16[8,12,12,896]{3,2,1,0:T(8,128)(2,1)S(1)} all-to-all(bf16[8,12,12,896]{3,2,1,0:T(8,128)(2,1)S(1)} %copy.112), channel_id=1, replica_groups=mesh['seq'=32,'mp_0'=4,'mp_1'=2] {'mp_0','mp_1'}, dimensions={0} | all-to-all | bytes 4128768 | tf_op jit(solution)/shard_map/all_to_all | solution.py:55
  200.2 6.1 %fusion.68 = (f32[12,12]{1,0:T(8,128)}, f32[12,12,896]{2,1,0:T(8,128)}) fusion(f32[12,12]{1,0:T(8,128)} %copy-done.6, bf16[12,12,896]{2,1,0:T(8,128)(2,1)S(1)} %gather_fusion.1, pred[12]{0:T(512)(128)(4,1)} %compare_and_fusion.1, f32[896]{0:T(1024)} %param.18, bf16[896,1792]{1,0:T(8,128)(2,1)S(1)} %copy-done, bf16[1792,896]{1,0:T(8,128)(2,1)} %param.20, ...), kind=kOutput, calls=%fused_computation.73 | convolution fusion | flops 928069504 | bytes 8749708 | tf_op jit(solution)/shard_map/nlf,ef->nle/dot_general | solution.py:100
  209.6 31.8 %all_to_all.16 = bf16[32,12,896]{2,1,0:T(8,128)(2,1)S(1)} all-to-all(bf16[32,12,896]{2,1,0:T(8,128)(2,1)S(1)} %copy.114), channel_id=1, replica_groups=mesh['seq'=32,'mp_0'=4,'mp_1'=2] {'seq'}, dimensions={0} | all-to-all | bytes 1376256 | tf_op jit(solution)/shard_map/all_to_all | solution.py:226
  (102 shorter events, 52.2 us)
Async XLA Ops:
  7.2 50.3 %copy-start = (bf16[896,1792]{1,0:T(8,128)(2,1)S(1)}, bf16[896,1792]{1,0:T(8,128)(2,1)}, u32[]{:S(2)}) copy-start(bf16[896,1792]{1,0:T(8,128)(2,1)} %param.19) | copy-start | bytes 9633796
  11.1 0.6 copy-start.15
  16.6 13.6 %copy-start.9 = (f32[2048]{0:T(1024)S(1)}, f32[2048]{0:T(1024)}, u32[]{:S(2)}) copy-start(f32[2048]{0:T(1024)} %param.17) | copy-start | bytes 24580
  16.6 37.4 %all-to-all-start = ((bf16[32,12,896]{2,1,0:T(8,128)(2,1)}), bf16[32,12,896]{2,1,0:T(8,128)(2,1)}, u32[]{:S(2)}, u32[]{:S(2)}) async-start(bf16[32,12,896]{2,1,0:T(8,128)(2,1)} %broadcast_select_fusion), calls=%async_computation | async-start | bytes 1835008 | tf_op jit(solution)/shard_map/all_to_all | solution.py:155
  28.2 214.2 %reduce-scatter.2.cloned.1.call-start = ((), (), s32[]{:S(2)}) async-start(), calls=%async_computation.4 | async-start | bytes 3538944 | tf_op jit(solution)/shard_map/reduce_scatter | solution.py:61
  28.4 4.9 %copy-start.18 = (pred[384]{0:T(512)(128)(4,1)}, pred[384]{0:T(512)(128)(4,1)S(1)}, u32[]{:S(2)}) copy-start(pred[384]{0:T(512)(128)(4,1)S(1)} %broadcast_in_dim.71) | copy-start | bytes 1156
  30.2 2.3 copy-start.7
  36.5 0.6 copy-start.12
  56.9 0.6 copy-start.6
  57.5 1.8 copy-start.11
  57.5 1.9 copy-start.17
  59.4 1.2 copy-start.3
  126.6 4.3 %copy-start.1 = (bf16[384,2048]{1,0:T(8,128)(2,1)S(1)}, bf16[384,2048]{1,0:T(8,128)(2,1)}, u32[]{:S(2)}) copy-start(bf16[384,2048]{1,0:T(8,128)(2,1)} %param.13) | copy-start | bytes 4718596
  126.6 4.3 %copy-start.4 = (bf16[2048,256]{1,0:T(8,128)(2,1)S(1)}, bf16[2048,256]{1,0:T(8,128)(2,1)}, u32[]{:S(2)}) copy-start(bf16[2048,256]{1,0:T(8,128)(2,1)} %param.21) | copy-start | bytes 3145732
  126.6 4.3 %copy-start.8 = (f32[384]{0:T(512)S(1)}, f32[384]{0:T(512)}, u32[]{:S(2)}) copy-start(f32[384]{0:T(512)} %copy-done.7) | copy-start | bytes 4612
  126.6 4.3 %copy-start.10 = (f32[2048]{0:T(1024)S(1)}, f32[2048]{0:T(1024)}, u32[]{:S(2)}) copy-start(f32[2048]{0:T(1024)} %param.17) | copy-start | bytes 24580
  151.1 2.1 copy-start.2
  151.1 2.1 copy-start.5
  206.3 2.2 copy-start.13
  209.4 32.0 %copy-start.14 = (pred[32]{0:T(512)(128)(4,1)S(1)}, pred[32]{0:T(512)(128)(4,1)}, u32[]{:S(2)}) copy-start(pred[32]{0:T(512)(128)(4,1)} %get-tuple-element.3) | copy-start | bytes 100
  209.4 32.0 %copy-start.16 = (s32[32]{0:T(128)S(1)}, s32[32]{0:T(128)}, u32[]{:S(2)}) copy-start(s32[32]{0:T(128)} %copy-done.15) | copy-start | bytes 388
Sparse Core Ops, SparseCore 0:
  134.6 33.3 reduce-scatter.1
where the time goes:
time: 252 us; the launch traced here: 251 us
  blocking collectives  105 us (42%)
  matrix products  44.9 us (18%)
  local copies, waits for them, and re-layouts  41 us (16%)
  other arithmetic  17.9 us (7%)
  waiting for transfers between devices  16.4 us (7%)
  between operations  14.4 us (6%)
  starting transfers between devices  11.6 us (5%)
    all_to_all x1, blocking collectives, summed_on_arrival(): tiles = lax.all_to_all(split_up(x, dim, devices), axis, 0, 0, tiled=True)  36.9 us
    all_gather x4, blocking collectives, gather_in_order(): tiles = lax.all_gather(tiles, axes[k], axis=0, tiled=True)  36.3 us
    all_to_all x1, blocking collectives, body(): lax.all_to_all(returned.astype(jnp.bfloat16), 'seq', split_axis=0, concat...  31.8 us
    all_to_all x1, waiting for transfers between devices, body(): lax.all_to_all(outgoing, 'seq', split_axis=0, concat_axis=0, tiled=True)  16.4 us
    all_to_all x1, starting transfers between devices, body(): lax.all_to_all(outgoing, 'seq', split_axis=0, concat_axis=0, tiled=True)  11.5 us
    dot_general x1, matrix products, encode_back(): jnp.einsum('nlf,ef->nle', grad_pre, w_in, preferred_element_type=jnp.floa...  6.08 us
  transfers between devices with their start and end apart: 2, of which 1 were waited for; matrix products, arithmetic and copies ran while one was open for 19% of the time, Pallas kernels for 0%

commit v1 on v0

--- a/solution.py
+++ b/solution.py
@@ -21,7 +21,9 @@
 def gather_in_order(x, axes, sequence):
     tiles = x[None]
     for k in sequence:
-        tiles = lax.all_gather(tiles, axes[k], axis=0, tiled=True)
+        tiles = jnp.concatenate(
+            lax.all_to_all(jnp.stack([tiles] * lax.axis_size(axes[k])), axes[k], 0, 0), axis=0
+        )
     block = [lax.axis_size(axes[k]) for k in reversed(sequence)]
     tiles = tiles.reshape(*block, *x.shape)
     turned = sorted(range(len(sequence)), key=lambda place: sequence[len(sequence) - 1 - place])

time: 252 us -> 278 us (1.10)
  blocking collectives: 105 us -> 80.5 us
  local copies, waits for them, and re-layouts: 41 us -> 64.7 us
  waiting for transfers between devices: 16.4 us -> 30.1 us
  starting transfers between devices: 11.6 us -> 20.2 us
    all_gather x4 -> x0, blocking collectives: 36.3 us -> none  [gather_in_order(): tiles = lax.all_gather(tiles, axes[k], axis=0, tiled=True)]
    all_to_all x0 -> x2, blocking collectives: none -> 10.1 us  [gather_in_order(): lax.all_to_all(jnp.stack([tiles] * lax.axis_size(axes[k])), axes[k], 0, 0)]
    all_to_all x0 -> x2, starting transfers between devices: none -> 8.53 us  [gather_in_order(): lax.all_to_all(jnp.stack([tiles] * lax.axis_size(axes[k])), axes[k], 0, 0)]
    another operation x0 -> x5, local copies, waits for them, and re-layouts: none -> 8.29 us  [the longest x4 4.86 us: gather_in_order(): jnp.stack([tiles] * lax.axis_size(axes[k]))]
    all_to_all x1, waiting for transfers between devices: 16.4 us -> 24.5 us  [body(): lax.all_to_all(outgoing, 'seq', split_axis=0, concat_axis=0, tiled=True)]
    all_to_all x0 -> x2, waiting for transfers between devices: none -> 5.51 us  [gather_in_order(): lax.all_to_all(jnp.stack([tiles] * lax.axis_size(axes[k])), axes[k], 0, 0)]
    reshape x0 -> x1, local copies, waits for them, and re-layouts: none -> 3.42 us  [gather_in_order(): tiles.transpose(*turned, *range(len(sequence), tiles.ndim))]
    all_to_all x0 -> x1, local copies, waits for them, and re-layouts: none -> 2.95 us  [gather_in_order(): lax.all_to_all(jnp.stack([tiles] * lax.axis_size(axes[k])), axes[k], 0, 0)]
  transfers between devices with their start and end apart: 2 -> 4, of which waited for: 1 -> 2; matrix products, arithmetic and copies ran while one was open for 19% -> 23% of each run, Pallas kernels for 0% -> 0%
where the time goes in v1:
time: 278 us; the launch traced here: 277 us
  blocking collectives  80.5 us (29%)
  local copies, waits for them, and re-layouts  64.7 us (23%)
  matrix products  46.2 us (17%)
  waiting for transfers between devices  30.1 us (11%)
  other arithmetic  20.5 us (7%)
  starting transfers between devices  20.2 us (7%)
  between operations  14.4 us (5%)
    all_to_all x1, blocking collectives, summed_on_arrival(): tiles = lax.all_to_all(split_up(x, dim, devices), axis, 0, 0, tiled=True)  38.6 us
    all_to_all x1, blocking collectives, body(): lax.all_to_all(returned.astype(jnp.bfloat16), 'seq', split_axis=0, concat...  31.8 us
    all_to_all x1, waiting for transfers between devices, body(): lax.all_to_all(outgoing, 'seq', split_axis=0, concat_axis=0, tiled=True)  24.5 us
    all_to_all x1, starting transfers between devices, body(): lax.all_to_all(outgoing, 'seq', split_axis=0, concat_axis=0, tiled=True)  11.4 us
    all_to_all x2, blocking collectives, gather_in_order(): lax.all_to_all(jnp.stack([tiles] * lax.axis_size(axes[k])), axes[k], 0, 0)  10.1 us
    all_to_all x2, starting transfers between devices, gather_in_order(): lax.all_to_all(jnp.stack([tiles] * lax.axis_size(axes[k])), axes[k], 0, 0)  8.53 us
    dot_general x1, matrix products, encode_back(): jnp.einsum('nlf,ef->nle', grad_pre, w_in, preferred_element_type=jnp.floa...  6.08 us
  transfers between devices with their start and end apart: 4, of which 2 were waited for; matrix products, arithmetic and copies ran while one was open for 23% of the time, Pallas kernels for 0%

profile of v1, /device:TPU:32, one launch (start us, length us, event | category | flops | bytes accessed | tf_op | source)
XLA Modules:
  0.0 276.5 jit_solution(403814047104822341)
XLA Ops:
  16.6 11.4 %all-to-all-start = ((bf16[32,12,896]{2,1,0:T(8,128)(2,1)}), bf16[32,12,896]{2,1,0:T(8,128)(2,1)}, u32[]{:S(2)}, u32[]{:S(2)}) async-start(bf16[32,12,896]{2,1,0:T(8,128)(2,1)} %broadcast_select_fusion), calls=%async_computation | async-start | bytes 1835008 | tf_op jit(solution)/shard_map/all_to_all | solution.py:157
  29.4 24.5 %all-to-all-done = bf16[32,12,896]{2,1,0:T(8,128)(2,1)} async-done(((bf16[32,12,896]{2,1,0:T(8,128)(2,1)}), bf16[32,12,896]{2,1,0:T(8,128)(2,1)}, u32[]{:S(2)}, u32[]{:S(2)}) %all-to-all-start) | async-done | bytes 688160 | tf_op jit(solution)/shard_map/all_to_all | solution.py:157
  60.5 4.7 %all_to_all.35 = bf16[2,1,6,12,896]{4,3,2,1,0:T(8,128)(2,1)} all-to-all(bf16[2,1,6,12,896]{4,3,2,1,0:T(8,128)(2,1)S(1)} %pad_maximum_fusion.2), channel_id=1, replica_groups=mesh['seq'=32,'mp_0'=4,'mp_1'=2] {'mp_1'}, dimensions={0} | all-to-all | bytes 516096 | tf_op jit(solution)/shard_map/all_to_all | solution.py:25
  66.2 4.3 %all-to-all-start.1 = ((bf16[4,1,6,12,896]{4,3,2,1,0:T(8,128)(2,1)}), bf16[4,1,6,12,896]{4,3,2,1,0:T(8,128)(2,1)}, u32[]{:S(2)}, u32[]{:S(2)}) async-start(bf16[4,1,6,12,896]{4,3,2,1,0:T(8,128)(2,1)} %stack.12), calls=%async_computation.1 | async-start | bytes 1376256 | tf_op jit(solution)/shard_map/all_to_all | solution.py:25
  76.7 5.5 %all-to-all-done.1 = bf16[4,1,6,12,896]{4,3,2,1,0:T(8,128)(2,1)} async-done(((bf16[4,1,6,12,896]{4,3,2,1,0:T(8,128)(2,1)}), bf16[4,1,6,12,896]{4,3,2,1,0:T(8,128)(2,1)}, u32[]{:S(2)}, u32[]{:S(2)}) %all-to-all-start.1) | async-done | bytes 516128 | tf_op jit(solution)/shard_map/all_to_all | solution.py:25
  84.4 5.4 %all_to_all.36 = bf16[2,4,6,12,896]{4,1,3,2,0:T(4,128)(2,1)} all-to-all(bf16[2,4,6,12,896]{4,1,3,2,0:T(4,128)(2,1)S(1)} %copy.123), channel_id=1, replica_groups=mesh['seq'=32,'mp_0'=4,'mp_1'=2] {'mp_1'}, dimensions={0} | all-to-all | bytes 2064384 | tf_op jit(solution)/shard_map/all_to_all | solution.py:25
  91.3 4.2 %all-to-all-start.4 = ((bf16[4,2,6,12,896]{4,1,3,2,0:T(2,128)(2,1)}), bf16[4,2,6,12,896]{4,1,3,2,0:T(2,128)(2,1)}, u32[]{:S(2)}, u32[]{:S(2)}) async-start(bf16[4,2,6,12,896]{4,1,3,2,0:T(2,128)(2,1)} %stack.15), calls=%async_computation.4 | async-start | bytes 2064384 | tf_op jit(solution)/shard_map/all_to_all | solution.py:25
  97.0 3.0 %fusion.47 = bf16[384,256]{1,0:T(8,128)(2,1)} fusion(bf16[2048,256]{1,0:T(8,128)(2,1)} %param.21, bf16[384,2048]{1,0:T(8,128)(2,1)} %param.13, f32[2048]{0:T(1024)} %param.17, f32[384]{0:T(512)S(1)} %add_rsqrt_fusion.1), kind=kOutput, calls=%fused_computation.54 | convolution fusion | flops 405897216 | bytes 2827776 | tf_op jit(solution)/shard_map/dot_general | solution.py:169
  101.7 3.0 %fusion.50 = bf16[384,256]{1,0:T(8,128)(2,1)} fusion(bf16[256,2048]{1,0:T(8,128)(2,1)} %param.24, bf16[384,2048]{1,0:T(8,128)(2,1)} %param.25, pred[384]{0:T(512)(128)(4,1)} %broadcast_in_dim.45), kind=kOutput, calls=%fused_computation.55 | convolution fusion | flops 403537920 | bytes 2818432 | tf_op jit(solution)/shard_map/dot_general | solution.py:80
  106.3 3.0 %copy.124 = bf16[4,2,6,12,896]{4,1,0,3,2:T(2,128)(2,1)} copy(bf16[4,2,6,12,896]{4,0,3,2,1:T(4,128)(2,1)} %bitcast.94) | data formatting | bytes 2064384 | tf_op jit(solution)/shard_map/transpose | solution.py:30
  109.4 3.4 %reshape.203 = bf16[8,6,12,896]{3,0,2,1:T(8,128)(2,1)} reshape(bf16[4,2,6,12,896]{4,1,0,3,2:T(2,128)(2,1)} %copy.124) | data formatting | bytes 2064384 | tf_op jit(solution)/shard_map/reshape | solution.py:30
  112.8 2.9 %copy.126 = bf16[4,2,6,12,896]{4,1,0,3,2:T(2,128)(2,1)} copy(bf16[4,2,6,12,896]{4,1,3,2,0:T(2,128)(2,1)} %all-to-all-done.4) | data formatting | bytes 2064384 | tf_op jit(solution)/shard_map/all_to_all | solution.py:25
  115.7 3.4 %reshape_reshape_reshape.3 = bf16[8,6,12,896]{3,0,2,1:T(8,128)(2,1)} reshape(bf16[4,2,6,12,896]{4,1,0,3,2:T(2,128)(2,1)} %copy.126) | data formatting | bytes 2064384 | tf_op jit(solution)/shard_map/reshape;reshape;reshape | solution.py:30
  122.9 4.6 %reshape.204 = bf16[12,96,896]{2,1,0:T(8,128)(2,1)} reshape(bf16[12,8,12,896]{3,2,1,0:T(8,128)(2,1)} %copy.127) | data formatting | bytes 4128768 | tf_op jit(solution)/shard_map/reshape | solution.py:36
  127.6 3.2 %convolution_convert_fusion = bf16[12,96,512]{2,1,0:T(8,128)(2,1)S(1)} fusion(bf16[12,96,896]{2,1,0:T(8,128)(2,1)} %reshape.204, bf16[896,256]{1,0:T(8,128)(2,1)} %param.23, bf16[896,256]{1,0:T(8,128)(2,1)} %param.22), kind=kOutput, calls=%fused_computation.36 | convolution fusion | flops 1059389440 | bytes 4161536 | tf_op jit(solution)/shard_map/nle,ef->nlf/dot_general | solution.py:160
  147.3 3.2 %fusion.54 = bf16[6,64,2,128]{3,1,2,0:T(8,128)(2,1)} fusion(f32[6,2,64,192]{3,2,1,0:T(8,128)} %fusion.87, f32[6,2,64,192]{3,2,1,0:T(8,128)} %fusion.78, bf16[6,192,2,128]{3,2,1,0:T(2,128)(2,1)} %reshape.207), kind=kOutput, calls=%fused_computation.59 | convolution fusion | flops 38585280 | bytes 1966080 | tf_op jit(solution)/shard_map/chqk,ckhd->cqhd/dot_general | solution.py:206
  158.3 3.3 %fusion.42 = bf16[6,192,2,128]{3,1,2,0:T(8,128)(2,1)} fusion(f32[6,2,64,192]{3,2,1,0:T(8,128)} %fusion.87, f32[6,2,64,192]{3,2,1,0:T(8,128)} %fusion.78, bf16[6,64,2,128]{3,2,1,0:T(2,128)(2,1)} %reshape.206), kind=kOutput, calls=%fused_computation.51 | convolution fusion | flops 38781888 | bytes 1966080 | tf_op jit(solution)/shard_map/chqk,cqhd->ckhd/dot_general | solution.py:210
  164.1 2.8 reshape.211
  166.8 2.8 %fusion.43 = bf16[6,192,2,128]{3,1,2,0:T(8,128)(2,1)} fusion(bf16[6,64,2,128]{3,2,1,0:T(2,128)(2,1)} %reshape.209, f32[6,2,64,192]{3,2,1,0:T(8,128)} %fusion.32), kind=kOutput, calls=%fused_computation.52 | convolution fusion | flops 38339520 | bytes 1376256 | tf_op jit(solution)/shard_map/chqk,cqhd->ckhd/dot_general | solution.py:202
  172.1 2.8 %reshape.212 = bf16[12,96,256]{2,1,0:T(8,128)(2,1)} reshape(bf16[6,192,2,128]{3,2,1,0:T(2,128)(2,1)} %copy.139) | data formatting | bytes 1179648 | tf_op jit(solution)/shard_map/reshape | solution.py:214
  179.1 4.6 %reshape.213 = bf16[12,8,12,896]{3,2,1,0:T(8,128)(2,1)} reshape(bf16[12,96,896]{2,1,0:T(8,128)(2,1)} %add_convert_fusion) | data formatting | bytes 4128768 | tf_op jit(solution)/shard_map/reshape | solution.py:51
  185.7 38.6 %all_to_all.37 = bf16[8,12,12,896]{3,2,1,0:T(8,128)(2,1)S(1)} all-to-all(bf16[8,12,12,896]{3,2,1,0:T(8,128)(2,1)S(1)} %copy.140), channel_id=1, replica_groups=mesh['seq'=32,'mp_0'=4,'mp_1'=2] {'mp_0','mp_1'}, dimensions={0} | all-to-all | bytes 4128768 | tf_op jit(solution)/shard_map/all_to_all | solution.py:57
  225.7 6.1 %fusion.68 = (f32[12,12]{1,0:T(8,128)}, f32[12,12,896]{2,1,0:T(8,128)}) fusion(f32[12,12]{1,0:T(8,128)} %copy-done.7, bf16[12,12,896]{2,1,0:T(8,128)(2,1)S(1)} %gather_fusion.1, pred[12]{0:T(512)(128)(4,1)} %compare_and_fusion.1, f32[896]{0:T(1024)} %param.18, bf16[896,1792]{1,0:T(8,128)(2,1)S(1)} %copy-done, bf16[1792,896]{1,0:T(8,128)(2,1)} %param.20, ...), kind=kOutput, calls=%fused_computation.74 | convolution fusion | flops 928069504 | bytes 8749708 | tf_op jit(solution)/shard_map/nlf,ef->nle/dot_general | solution.py:102
  235.1 31.8 %all_to_all.38 = bf16[32,12,896]{2,1,0:T(8,128)(2,1)S(1)} all-to-all(bf16[32,12,896]{2,1,0:T(8,128)(2,1)S(1)} %copy.142), channel_id=1, replica_groups=mesh['seq'=32,'mp_0'=4,'mp_1'=2] {'seq'}, dimensions={0} | all-to-all | bytes 1376256 | tf_op jit(solution)/shard_map/all_to_all | solution.py:228
  (111 shorter events, 79.6 us)
Async XLA Ops:
  7.2 50.2 %copy-start = (bf16[896,1792]{1,0:T(8,128)(2,1)S(1)}, bf16[896,1792]{1,0:T(8,128)(2,1)}, u32[]{:S(2)}) copy-start(bf16[896,1792]{1,0:T(8,128)(2,1)} %param.19) | copy-start | bytes 9633796
  11.1 0.6 copy-start.15
  16.6 37.3 %all-to-all-start = ((bf16[32,12,896]{2,1,0:T(8,128)(2,1)}), bf16[32,12,896]{2,1,0:T(8,128)(2,1)}, u32[]{:S(2)}, u32[]{:S(2)}) async-start(bf16[32,12,896]{2,1,0:T(8,128)(2,1)} %broadcast_select_fusion), calls=%async_computation | async-start | bytes 1835008 | tf_op jit(solution)/shard_map/all_to_all | solution.py:157
  28.2 0.6 copy-start.12
  56.7 0.6 copy-start.7
  57.3 1.8 copy-start.11
  57.3 1.9 copy-start.17
  59.3 1.2 copy-start.3
  66.2 16.1 %all-to-all-start.1 = ((bf16[4,1,6,12,896]{4,3,2,1,0:T(8,128)(2,1)}), bf16[4,1,6,12,896]{4,3,2,1,0:T(8,128)(2,1)}, u32[]{:S(2)}, u32[]{:S(2)}) async-start(bf16[4,1,6,12,896]{4,3,2,1,0:T(8,128)(2,1)} %stack.12), calls=%async_computation.1 | async-start | bytes 1376256 | tf_op jit(solution)/shard_map/all_to_all | solution.py:25
  83.8 5.9 %copy-start.5 = (bf16[2,6,12,896]{3,0,2,1:T(2,128)(2,1)S(1)}, bf16[2,6,12,896]{3,0,2,1:T(2,128)(2,1)}, u32[]{:S(2)}) copy-start(bf16[2,6,12,896]{3,0,2,1:T(2,128)(2,1)} %copy.125) | copy-start | bytes 774148
  91.3 21.5 %all-to-all-start.4 = ((bf16[4,2,6,12,896]{4,1,3,2,0:T(2,128)(2,1)}), bf16[4,2,6,12,896]{4,1,3,2,0:T(2,128)(2,1)}, u32[]{:S(2)}, u32[]{:S(2)}) async-start(bf16[4,2,6,12,896]{4,1,3,2,0:T(2,128)(2,1)} %stack.15), calls=%async_computation.4 | async-start | bytes 2064384 | tf_op jit(solution)/shard_map/all_to_all | solution.py:25
  95.5 172.3 %reduce-scatter.2.cloned.1.call-start = ((), (), s32[]{:S(2)}) async-start(), calls=%async_computation.8 | async-start | bytes 3538944 | tf_op jit(solution)/shard_map/reduce_scatter | solution.py:63
  96.4 0.6 copy-start.8
  150.5 4.3 %copy-start.1 = (bf16[384,2048]{1,0:T(8,128)(2,1)S(1)}, bf16[384,2048]{1,0:T(8,128)(2,1)}, u32[]{:S(2)}) copy-start(bf16[384,2048]{1,0:T(8,128)(2,1)} %param.13) | copy-start | bytes 4718596
  150.5 4.3 %copy-start.4 = (bf16[2048,256]{1,0:T(8,128)(2,1)S(1)}, bf16[2048,256]{1,0:T(8,128)(2,1)}, u32[]{:S(2)}) copy-start(bf16[2048,256]{1,0:T(8,128)(2,1)} %param.21) | copy-start | bytes 3145732
  150.5 4.3 %copy-start.9 = (f32[384]{0:T(512)S(1)}, f32[384]{0:T(512)}, u32[]{:S(2)}) copy-start(f32[384]{0:T(512)} %copy-done.8) | copy-start | bytes 4612
  150.5 4.3 %copy-start.10 = (f32[2048]{0:T(1024)S(1)}, f32[2048]{0:T(1024)}, u32[]{:S(2)}) copy-start(f32[2048]{0:T(1024)} %param.17) | copy-start | bytes 24580
  174.9 2.1 copy-start.2
  174.9 2.1 copy-start.6
  231.8 2.2 copy-start.13
  234.8 32.0 %copy-start.14 = (pred[32]{0:T(512)(128)(4,1)S(1)}, pred[32]{0:T(512)(128)(4,1)}, u32[]{:S(2)}) copy-start(pred[32]{0:T(512)(128)(4,1)} %get-tuple-element.3) | copy-start | bytes 100
  234.9 32.0 %copy-start.16 = (s32[32]{0:T(128)S(1)}, s32[32]{0:T(128)}, u32[]{:S(2)}) copy-start(s32[32]{0:T(128)} %copy-done.15) | copy-start | bytes 388
Sparse Core Ops, SparseCore 0:
  158.4 34.9 reduce-scatter.1
